TPU v7x, 32 devices: a whole 2x2x4 slice. The times are simulated.
32 devices in a mesh: pairs: 2 (over x), ctx: 16 (over z, y, core).
Axes of the slice: x: 2, y: 2, z: 4, core: 2. Of those that a mesh axis runs over, the one named last changes fastest.
Arguments:
- prompt_keys: bfloat16 [1024, 512], P(('pairs', 'ctx')), parts along dimension 0, may hold values from -4 to 4
- prompt_values: bfloat16 [1024, 512], P(('pairs', 'ctx')), parts along dimension 0, may hold values from -6 to 6
- queries: bfloat16 [4, 768, 4096], P('pairs', 'ctx'), parts along dimension 0, may hold values from -100 to 100
- resp_keys: bfloat16 [4, 768, 512], P('pairs', 'ctx'), parts along dimension 0, may hold values from -6 to 6
- resp_values: bfloat16 [4, 768, 512], P('pairs', 'ctx'), parts along dimension 0, may hold values from -6 to 6
- cotangent: bfloat16 [4, 768, 4096], P('pairs', 'ctx'), parts along dimension 0, may hold values from -48 to 48
- lengths: int32 [4], P('pairs'), parts along dimension 0, may hold values from 192 to 768, as said below
Outputs:
- grad_queries: float32 [4, 768, 4096], P('pairs', 'ctx'), parts along dimension 0
- grad_resp_keys: float32 [4, 768, 512], P('pairs', 'ctx'), parts along dimension 0
- grad_resp_values: float32 [4, 768, 512], P('pairs', 'ctx'), parts along dimension 0
- grad_prompt_keys: float32 [1024, 512], P(('pairs', 'ctx')), parts along dimension 0
- grad_prompt_values: float32 [1024, 512], P(('pairs', 'ctx')), parts along dimension 0
There are 2 independent parts, one for each index of `pairs`. A program takes and returns all parts, laid end to end along the dimension named above; each array names one. Nothing has to cross between parts.
Inputs may be any that keep to these rules, and one draw needn't show every extreme that they name: `lengths`: in every pair one of the two responses has all 768 rows live.
All inputs are finite; a program needn't handle non-finite values.
Results may differ from a plain program's by a relative error of at most 0.005.
Values may be sent and summed in bfloat16 or wider, within the bound.
A program may use at most 128 MiB of HBM per device.

v0:
```python
import functools

import jax
import jax.numpy as jnp
from jax import lax
from jax.experimental import pallas as pl
from jax.experimental.pallas import tpu as pltpu
from jax.sharding import PartitionSpec as P

HEAD_DIM = 128
SCALE = HEAD_DIM ** (-0.5)
LOG2E = 1.4426950408889634
MIB = 1024 * 1024


def chip_of(pos, n):
    high = pos // (n // 2)
    return (1 - high) * (2 * pos) + high * (2 * (n - 1 - pos) + 1)


def place(n):
    me = lax.axis_index("ctx")
    core, chip = me % 2, me // 2
    odd = chip % 2
    pos = (1 - odd) * (chip // 2) + odd * (n - 1 - chip // 2)
    partner = 2 * chip + 1 - core
    right = 2 * chip_of((pos + 1) % n, n) + core
    left = 2 * chip_of((pos + n - 1) % n, n) + core
    return core, chip, pos, partner, (right, left)


def greet(partner, sides):
    barrier = pltpu.get_barrier_semaphore()
    for other in (partner,) + sides:
        pl.semaphore_signal(
            barrier, inc=1, device_id={"ctx": other}, device_id_type=pl.DeviceIdType.MESH
        )
    pl.semaphore_wait(barrier, 3)


def steps_of(n):
    far, near = n // 2, n - 1 - n // 2
    return ((far, near), (near, far))


def remote(src, dst, send, recv, device):
    return pltpu.make_async_remote_copy(
        src_ref=src,
        dst_ref=dst,
        send_sem=send,
        recv_sem=recv,
        device_id={"ctx": device},
        device_id_type=pl.DeviceIdType.MESH,
    )


def fused_kernel(
    n, block, lengths, pk, pv, rk, rv, q, u,
    gq, grk, grv, gpk, gpv,
    kp, kr, qh, uh, qs, us, s_buf, d_buf, qt_buf, m_buf, l_buf, e_buf,
    tp, tr, sp, sr, rp, rr, fp, fr, dq,
    gsend, grecv, ssend, srecv, isend, irecv, ilocal, qsend, qrecv, qlocal,
    osend, orecv, olocal,
):
    core, chip, pos, partner, sides = place(n)
    prows, rrows = pk.shape[0], rk.shape[1]
    wide = q.shape[2] // 2
    heads = kp.shape[1]
    group = wide // HEAD_DIM // heads
    units = [(k, b) for k in range(heads) for b in range(2)]
    hops = steps_of(n)
    flows = ((0, 0), (1, 1), (0, 1), (1, 0))
    inputs = ((pk, rk), (pv, rv))
    outputs = ((gpk, grk), (gpv, grv))

    def head_columns(owner, k):
        return pl.ds(pl.multiple_of((owner * heads + k) * HEAD_DIM, HEAD_DIM), HEAD_DIM)

    def parts_in(unit):
        return (0, 1) if units[unit][1] == 0 else (1,)

    def parts_out(unit):
        return (1,) if units[unit][1] == 0 else (0, 1)

    def rows_of(where, size):
        return pl.ds(pl.multiple_of(where * size, 16), size)

    def gathered(kind, unit, part, rows):
        k, b = units[unit]
        return kp.at[kind, k, rows, :] if part == 0 else kr.at[kind, k, b, rows, :]

    def given(kind, unit, part, cols):
        ref = inputs[kind][part]
        return ref.at[:, cols] if part == 0 else ref.at[units[unit][1], :, cols]

    greet(partner, sides)
    entries = []
    for unit in range(len(units)):
        k = units[unit][0]
        for part in parts_in(unit):
            size = prows if part == 0 else rrows
            own = rows_of(chip * 2 + core, size)
            for kind in range(2):
                at = (kind, unit, part)
                away = remote(
                    given(kind, unit, part, head_columns(1 - core, k)),
                    gathered(kind, unit, part, own), isend.at[at], irecv.at[at], partner,
                )
                away.start()
                stay = pltpu.make_async_copy(
                    given(kind, unit, part, head_columns(core, k)),
                    gathered(kind, unit, part, own), ilocal.at[at],
                )
                stay.start()
                entries.append((unit, away, stay))
    wide_own = pl.ds(pl.multiple_of(core * wide, wide), wide)
    wide_far = pl.ds(pl.multiple_of((1 - core) * wide, wide), wide)
    query_moves = []
    for i, (src, dst) in enumerate(((q, qh), (u, uh))):
        away = remote(src.at[:, :, wide_far], dst.at[1], qsend.at[i], qrecv.at[i], partner)
        away.start()
        stay = pltpu.make_async_copy(src.at[:, :, wide_own], dst.at[0], qlocal.at[i])
        stay.start()
        query_moves += [away, stay]

    moved = {}

    def pull(unit, t):
        if t == 1:
            for owner, away, stay in entries:
                if owner == unit:
                    away.wait_recv()
                    stay.wait()
        for part in parts_in(unit):
            size = 2 * (prows if part == 0 else rrows)
            for way, kind in flows:
                if t > hops[way][kind]:
                    continue
                if t > 1:
                    moved[unit, t - 1, part, way, kind].wait_recv()
                origin = (pos + n - (t - 1)) % n if way == 0 else (pos + t - 1) % n
                ref = gathered(kind, unit, part, rows_of(chip_of(origin, n), size))
                at = (way, kind, unit, part, t - 1)
                copy = remote(ref, ref, gsend.at[at], grecv.at[at], sides[way])
                copy.start()
                moved[unit, t, part, way, kind] = copy

    def pulled(unit):
        for part in parts_in(unit):
            for way, kind in flows:
                moved[unit, hops[way][kind], part, way, kind].wait_recv()

    sent = {}

    def term(kind, unit, part, where):
        k, b = units[unit]
        if part == 0:
            return tp[kind, k, rows_of(where, 2 * prows), :]
        return tr[kind, k, b, rows_of(where, 2 * rrows), :]

    def slot(bufs, part, way, kind, unit, t):
        k = units[unit][0]
        if part == 0:
            return bufs[0].at[way, kind, k, t - 1]
        return bufs[1].at[way, kind, unit, t - 1]

    def push(unit, t, part):
        for way, kind in flows:
            total = hops[way][kind]
            if t > total:
                continue
            away = total - t + 1
            target = (pos + away) % n if way == 0 else (pos + n - away) % n
            value = term(kind, unit, part, chip_of(target, n))
            if t > 1:
                sent[unit, t - 1, part, way, kind].wait_recv()
                value = value + slot((rp, rr), part, way, kind, unit, t - 1)[...].astype(jnp.float32)
            src = slot((sp, sr), part, way, kind, unit, t)
            src[...] = value.astype(jnp.bfloat16)
            at = (way, kind, unit, part, t - 1)
            copy = remote(
                src, slot((rp, rr), part, way, kind, unit, t), ssend.at[at], srecv.at[at], sides[way]
            )
            copy.start()
            sent[unit, t, part, way, kind] = copy

    outgoing = []

    def finish(unit, part):
        k, b = units[unit]
        size = prows if part == 0 else rrows
        for kind in range(2):
            value = term(kind, unit, part, chip)
            for way in range(2):
                last = hops[way][kind]
                sent[unit, last, part, way, kind].wait_recv()
                value = value + slot((rp, rr), part, way, kind, unit, last)[...].astype(jnp.float32)
            final = fp.at[kind, k] if part == 0 else fr.at[kind, k, b]
            final[...] = value
            out = outputs[kind][part]
            cols = head_columns(core, k)
            dst = out.at[:, cols] if part == 0 else out.at[b, :, cols]
            at = (kind, unit, part)
            away = remote(
                final.at[rows_of(1 - core, size), :], dst, osend.at[at], orecv.at[at], partner
            )
            away.start()
            stay = pltpu.make_async_copy(final.at[rows_of(core, size), :], dst, olocal.at[at])
            stay.start()
            outgoing.extend((away, stay))

    half = group * rrows
    lanes = 2 * half
    prompt_blocks = kp.shape[2] // block
    resp_blocks = kr.shape[3] // block
    base = chip * 2 * rrows
    factor = SCALE * LOG2E
    lane = lax.broadcasted_iota(jnp.int32, (1, lanes), 1)
    row_of = lax.rem(lane, rrows)
    positions = base + row_of + rrows * jnp.where(lane < half, core, 1 - core)
    key_iota = lax.broadcasted_iota(jnp.int32, (block, 1), 0)
    row_iota = lax.broadcasted_iota(jnp.int32, (rrows, 1), 0)
    nt = (((1,), (1,)), ((), ()))

    def key_rows(j):
        return pl.ds(pl.multiple_of(j * block, block), block)

    def compute(unit, ticks):
        k, b = units[unit]
        length = lengths[b]
        for source in range(2):
            owner = core if source == 0 else 1 - core
            live = base + owner * rrows + row_iota < length
            for g in range(group):
                cols = pl.ds((k * group + g) * HEAD_DIM, HEAD_DIM)
                at = pl.ds(source * half + g * rrows, rrows)
                qs[at, :] = qh[source, b, :, cols]
                rows = uh[source, b, :, cols]
                us[at, :] = jnp.where(live, rows, jnp.zeros_like(rows))
        m_buf[...] = jnp.full_like(m_buf, -jnp.inf)
        l_buf[...] = jnp.zeros_like(l_buf)
        e_buf[...] = jnp.zeros_like(e_buf)
        qt_buf[...] = jnp.zeros_like(qt_buf)
        ticks(0)

        def scores(keys, at, j, causal):
            s = lax.dot_general(keys, qs[...], nt, preferred_element_type=jnp.float32)
            if causal:
                s = jnp.where(key_iota + j * block <= positions, s, -jnp.inf)
            s_buf[at, :] = s
            m_buf[...] = jnp.maximum(m_buf[...], jnp.max(s, axis=0, keepdims=True))

        @pl.loop(0, prompt_blocks)
        def _(j):
            scores(kp[0, k, key_rows(j), :], key_rows(j), j, False)

        ticks(1)

        @pl.loop(0, resp_blocks)
        def _(j):
            scores(kr[0, k, b, key_rows(j), :], key_rows(prompt_blocks + j), j, True)

        ticks(2)
        shift = m_buf[...] * factor

        def weights(vals, at):
            p = jnp.exp2(s_buf[at, :] * factor - shift)
            d = lax.dot_general(vals, us[...], nt, preferred_element_type=jnp.float32)
            l_buf[...] += jnp.sum(p, axis=0, keepdims=True)
            e_buf[...] += jnp.sum(p * d, axis=0, keepdims=True)
            s_buf[at, :] = p
            d_buf[at, :] = d

        @pl.loop(0, prompt_blocks)
        def _(j):
            weights(kp[1, k, key_rows(j), :], key_rows(j))

        ticks(3)

        @pl.loop(0, resp_blocks)
        def _(j):
            weights(kr[1, k, b, key_rows(j), :], key_rows(prompt_blocks + j))

        ticks(4)
        inverse = 1.0 / l_buf[...]
        delta = e_buf[...] * inverse

        def grads(keys, at):
            p = s_buf[at, :] * inverse
            ds = (p * (d_buf[at, :] - delta)).astype(jnp.bfloat16)
            dv = jnp.dot(p.astype(jnp.bfloat16), us[...], preferred_element_type=jnp.float32)
            dk = jnp.dot(ds, qs[...], preferred_element_type=jnp.float32) * SCALE
            qt_buf[...] += jnp.dot(keys.T, ds, preferred_element_type=jnp.float32)
            return dk, dv

        @pl.loop(0, prompt_blocks)
        def _(j):
            at = key_rows(j)
            pair = grads(kp[0, k, at, :], at)
            for kind in range(2):
                if b == 0:
                    tp[kind, k, at, :] = pair[kind]
                else:
                    tp[kind, k, at, :] += pair[kind]

        ticks(5)

        @pl.loop(0, resp_blocks)
        def _(j):
            at = key_rows(j)
            pair = grads(kr[0, k, b, at, :], key_rows(prompt_blocks + j))
            for kind in range(2):
                tr[kind, k, b, at, :] = pair[kind]

        ticks(6)
        result = qt_buf[...].T * SCALE
        for source in range(2):
            for g in range(group):
                start = source * half + g * rrows
                dq[source, b, :, pl.ds((k * group + g) * HEAD_DIM, HEAD_DIM)] = result[
                    start : start + rrows
                ]
        span = group * HEAD_DIM
        cols = pl.ds(k * span, span)
        to = pl.ds(pl.multiple_of(core * wide + k * span, span), span)
        i = 2 + unit
        away = remote(dq.at[1, b, :, cols], gq.at[b, :, to], qsend.at[i], qrecv.at[i], partner)
        away.start()
        stay = pltpu.make_async_copy(dq.at[0, b, :, cols], gq.at[b, :, to], qlocal.at[i])
        stay.start()
        outgoing.extend((away, stay))

    last = len(units) - 1
    far = n // 2
    pulls = [(unit, t) for unit in range(1, last + 1) for t in range(1, far + 1)]

    def advance(count):
        for _ in range(min(count, len(pulls))):
            pull(*pulls.pop(0))

    pull(0, 1)
    for copy in query_moves:
        copy.wait()
    for t in range(2, far + 1):
        pull(0, t)
        advance(1)
    pulled(0)

    for unit in range(last + 1):
        pushes = []
        if unit > 0:
            pushes = [(unit - 1, t) for t in range(1, far + 1)]

        def ticks(at, unit=unit, pushes=pushes):
            due = -(-far // 3)
            if at in (0, 2, 4, 6):
                for _ in range(-(-far // 4)):
                    if pushes:
                        which, t = pushes.pop(0)
                        for part in reversed(parts_out(which)):
                            push(which, t, part)
            if at in (1, 3, 5):
                advance(due)
            if at == 0 and unit > 1:
                for part in parts_out(unit - 2):
                    finish(unit - 2, part)
            if at == 5 and unit == last:
                push(unit, 1, 0)

        compute(unit, ticks)
        if unit < last:
            while pulls and pulls[0][0] <= unit + 1:
                advance(1)
            pulled(unit + 1)
    for t in range(1, far + 1):
        push(last, t, 1)
        if t > 1:
            push(last, t, 0)
        if t == 1:
            for part in parts_out(last - 1):
                finish(last - 1, part)
    finish(last, 0)
    finish(last, 1)
    for copy in moved.values():
        copy.wait_send()
    for copy in sent.values():
        copy.wait_send()
    for _, away, _ in entries:
        away.wait_send()
    for copy in outgoing:
        copy.wait()


def key_block(prompt, resp):
    size = 256
    while prompt % size or resp % size:
        size //= 2
    return size


def local(prompt_keys, prompt_values, queries, resp_keys, resp_values, cotangent, lengths):
    devices = lax.axis_size("ctx")
    n = devices // 2
    prows, columns = prompt_keys.shape
    rows, wide = queries.shape[1], queries.shape[2] // 2
    heads = columns // 2 // HEAD_DIM
    prompt, resp = prows * devices, rows * devices
    smem = pl.BlockSpec(memory_space=pltpu.SMEM)
    hbm = pl.BlockSpec(memory_space=pl.ANY)
    shape = jax.ShapeDtypeStruct
    bf16, f32 = jnp.bfloat16, jnp.float32
    vmem, dma = pltpu.VMEM, pltpu.SemaphoreType.DMA
    hop, units = n // 2, 2 * heads
    block = key_block(prompt, resp)
    lanes = 2 * rows * (wide // HEAD_DIM) // heads
    total = prompt + resp
    gq, grk, grv, gpk, gpv = pl.pallas_call(
        functools.partial(fused_kernel, n, block),
        out_shape=(
            shape((2, rows, 2 * wide), f32),
            shape((2, rows, columns), f32), shape((2, rows, columns), f32),
            shape((prows, columns), f32), shape((prows, columns), f32),
        ),
        in_specs=[smem] + [hbm] * 6,
        out_specs=(hbm,) * 5,
        scratch_shapes=[
            vmem((2, heads, prompt, HEAD_DIM), bf16),
            vmem((2, heads, 2, resp, HEAD_DIM), bf16),
            vmem((2, 2, rows, wide), bf16), vmem((2, 2, rows, wide), bf16),
            vmem((lanes, HEAD_DIM), bf16), vmem((lanes, HEAD_DIM), bf16),
            vmem((total, lanes), f32), vmem((total, lanes), f32),
            vmem((HEAD_DIM, lanes), f32),
            vmem((1, lanes), f32), vmem((1, lanes), f32), vmem((1, lanes), f32),
            vmem((2, heads, prompt, HEAD_DIM), f32),
            vmem((2, heads, 2, resp, HEAD_DIM), f32),
            vmem((2, 2, heads, hop, 2 * prows, HEAD_DIM), bf16),
            vmem((2, 2, units, hop, 2 * rows, HEAD_DIM), bf16),
            vmem((2, 2, heads, hop, 2 * prows, HEAD_DIM), bf16),
            vmem((2, 2, units, hop, 2 * rows, HEAD_DIM), bf16),
            vmem((2, heads, 2 * prows, HEAD_DIM), f32),
            vmem((2, heads, 2, 2 * rows, HEAD_DIM), f32),
            vmem((2, 2, rows, wide), f32),
            dma((2, 2, units, 2, hop)), dma((2, 2, units, 2, hop)),
            dma((2, 2, units, 2, hop)), dma((2, 2, units, 2, hop)),
            dma((2, units, 2)), dma((2, units, 2)), dma((2, units, 2)),
            dma((2 + units,)), dma((2 + units,)), dma((2 + units,)),
            dma((2, units, 2)), dma((2, units, 2)), dma((2, units, 2)),
        ],
        compiler_params=pltpu.CompilerParams(
            collective_id=0, has_side_effects=True, vmem_limit_bytes=60 * MIB
        ),
        name="fused",
    )(lengths, prompt_keys, prompt_values, resp_keys, resp_values, queries, cotangent)
    return gq, grk, grv, gpk, gpv


def solution(mesh):
    placed = (
        P(("pairs", "ctx"), None),
        P(("pairs", "ctx"), None),
        P("pairs", "ctx", None),
        P("pairs", "ctx", None),
        P("pairs", "ctx", None),
        P("pairs", "ctx", None),
        P("pairs"),
    )
    return jax.shard_map(
        local,
        mesh=mesh,
        in_specs=placed,
        out_specs=(
            P("pairs", "ctx", None),
            P("pairs", "ctx", None),
            P("pairs", "ctx", None),
            P(("pairs", "ctx"), None),
            P(("pairs", "ctx"), None),
        ),
        check_vma=False,
    )
```

profile of v0, /device:TPU:3, one launch (start us, length us, event | category | flops | bytes accessed | tf_op | source)
XLA Modules:
  0.0 87.1 jit_solution(14590826034855585398)
XLA Ops:
  0.6 81.1 %fused.1 = (f32[2,48,4096]{2,1,0:T(8,128)}, f32[2,48,512]{2,1,0:T(8,128)}, f32[2,48,512]{2,1,0:T(8,128)}, f32[32,512]{1,0:T(8,128)}, f32[32,512]{1,0:T(8,128)}) custom-call(s32[2]{0:T(128)} %lengths.1, bf16[32,512]{1,0:T(8,128)(2,1)} %pk.1, bf16[32,512]{1,0:T(8,128)(2,1)} %pv.1, bf16[2,48,512]{2,1,0:T(8,128)(2,1)} %rk.1, bf16[2,48,512]{2,1,0:T(8,128)(2,1)} %rv.1, ...), custom_call_target="tpu_custom_call" | custom-call | tf_op jit(solution)/shard_map/fused/pallas_call | solution.py:417
  81.7 0.0 copy-start.1
  81.7 0.0 copy-start
  81.8 0.0 copy-start.3
  81.8 0.0 copy-start.2
  81.8 2.7 %copy.17 = f32[2,48,4096]{2,1,0:T(8,128)} copy(f32[2,48,4096]{2,1,0:T(8,128)} %get-tuple-element.10) | data formatting | bytes 3145728
  84.5 0.0 copy-done.1
  84.5 0.7 copy.18
  85.2 0.0 copy-done
  85.2 0.7 copy.19
  85.8 0.0 copy-done.3
  85.8 0.6 copy.20
  86.5 0.0 copy-done.2
  86.5 0.6 copy.21
Async XLA Ops:
  81.7 2.8 %copy-start.1 = (f32[2,48,512]{2,1,0:T(8,128)S(1)}, f32[2,48,512]{2,1,0:T(8,128)}, u32[]{:S(2)}) copy-start(f32[2,48,512]{2,1,0:T(8,128)} %get-tuple-element.11) | copy-start | bytes 589828
  81.7 3.4 %copy-start = (f32[2,48,512]{2,1,0:T(8,128)S(1)}, f32[2,48,512]{2,1,0:T(8,128)}, u32[]{:S(2)}) copy-start(f32[2,48,512]{2,1,0:T(8,128)} %get-tuple-element.12) | copy-start | bytes 589828
  81.8 4.1 %copy-start.3 = (f32[32,512]{1,0:T(8,128)S(1)}, f32[32,512]{1,0:T(8,128)}, u32[]{:S(2)}) copy-start(f32[32,512]{1,0:T(8,128)} %get-tuple-element.13) | copy-start | bytes 196612
  81.8 4.7 %copy-start.2 = (f32[32,512]{1,0:T(8,128)S(1)}, f32[32,512]{1,0:T(8,128)}, u32[]{:S(2)}) copy-start(f32[32,512]{1,0:T(8,128)} %get-tuple-element.14) | copy-start | bytes 196612
where the time goes:
time: 88.3 us; the launch traced here: 87.1 us
  Pallas kernels  81.1 us (92%)
  local copies, waits for them, and re-layouts  5.34 us (6%)
    pallas_call x1, Pallas kernels, local(): pl.pallas_call(functools.partial(fused_kernel, n, block), out_shape=(shap...  81.1 us
    unnamed x13, local copies, waits for them, and re-layouts  5.34 us

commit v1 on v0

--- a/solution.py
+++ b/solution.py
@@ -11,6 +11,7 @@
 SCALE = HEAD_DIM ** (-0.5)
 LOG2E = 1.4426950408889634
 MIB = 1024 * 1024
+TICKS = 7
 
 
 def chip_of(pos, n):
@@ -250,13 +251,13 @@
             s_buf[at, :] = s
             m_buf[...] = jnp.maximum(m_buf[...], jnp.max(s, axis=0, keepdims=True))
 
-        @pl.loop(0, prompt_blocks)
+        @pl.loop(0, prompt_blocks, unroll=True)
         def _(j):
             scores(kp[0, k, key_rows(j), :], key_rows(j), j, False)
 
         ticks(1)
 
-        @pl.loop(0, resp_blocks)
+        @pl.loop(0, resp_blocks, unroll=True)
         def _(j):
             scores(kr[0, k, b, key_rows(j), :], key_rows(prompt_blocks + j), j, True)
 
@@ -271,13 +272,13 @@
             s_buf[at, :] = p
             d_buf[at, :] = d
 
-        @pl.loop(0, prompt_blocks)
+        @pl.loop(0, prompt_blocks, unroll=True)
         def _(j):
             weights(kp[1, k, key_rows(j), :], key_rows(j))
 
         ticks(3)
 
-        @pl.loop(0, resp_blocks)
+        @pl.loop(0, resp_blocks, unroll=True)
         def _(j):
             weights(kr[1, k, b, key_rows(j), :], key_rows(prompt_blocks + j))
 
@@ -293,7 +294,7 @@
             qt_buf[...] += jnp.dot(keys.T, ds, preferred_element_type=jnp.float32)
             return dk, dv
 
-        @pl.loop(0, prompt_blocks)
+        @pl.loop(0, prompt_blocks, unroll=True)
         def _(j):
             at = key_rows(j)
             pair = grads(kp[0, k, at, :], at)
@@ -305,7 +306,7 @@
 
         ticks(5)
 
-        @pl.loop(0, resp_blocks)
+        @pl.loop(0, resp_blocks, unroll=True)
         def _(j):
             at = key_rows(j)
             pair = grads(kr[0, k, b, at, :], key_rows(prompt_blocks + j))
@@ -332,53 +333,61 @@
 
     last = len(units) - 1
     far = n // 2
-    pulls = [(unit, t) for unit in range(1, last + 1) for t in range(1, far + 1)]
+    pulls = [(w - t + 1, t) for w in range(last + far) for t in range(1, far + 1) if 0 <= w - t + 1 <= last]
+    pulls.sort(key=lambda hop: (hop[0] + hop[1], hop[1]))
 
     def advance(count):
         for _ in range(min(count, len(pulls))):
             pull(*pulls.pop(0))
 
-    pull(0, 1)
+    first = pulls.index((0, far)) + 1
+    advance(1)
     for copy in query_moves:
         copy.wait()
-    for t in range(2, far + 1):
-        pull(0, t)
-        advance(1)
+    advance(first - 1)
     pulled(0)
-
+    per_tick = -(-len(pulls) // 6)
+    due = {}
+    for unit in range(last):
+        for t in range(1, far + 1):
+            when = (unit + 1) * TICKS + (t - 1) * 12 // far
+            due.setdefault(min(when, (last + 1) * TICKS), []).append((unit, t))
+
+    def push_all(unit, t):
+        for part in reversed(parts_out(unit)):
+            push(unit, t, part)
+        if t == far:
+            closing.append(unit)
+
+    closing = []
     for unit in range(last + 1):
-        pushes = []
-        if unit > 0:
-            pushes = [(unit - 1, t) for t in range(1, far + 1)]
-
-        def ticks(at, unit=unit, pushes=pushes):
-            due = -(-far // 3)
-            if at in (0, 2, 4, 6):
-                for _ in range(-(-far // 4)):
-                    if pushes:
-                        which, t = pushes.pop(0)
-                        for part in reversed(parts_out(which)):
-                            push(which, t, part)
-            if at in (1, 3, 5):
-                advance(due)
-            if at == 0 and unit > 1:
-                for part in parts_out(unit - 2):
-                    finish(unit - 2, part)
+
+        def ticks(at, unit=unit):
+            for which, t in due.get(unit * TICKS + at, []):
+                push_all(which, t)
+            if at > 0:
+                advance(per_tick)
             if at == 5 and unit == last:
                 push(unit, 1, 0)
 
         compute(unit, ticks)
         if unit < last:
-            while pulls and pulls[0][0] <= unit + 1:
+            while any(hop[0] <= unit + 1 for hop in pulls):
                 advance(1)
             pulled(unit + 1)
-    for t in range(1, far + 1):
+    push(last, 1, 1)
+    for which, t in due.get((last + 1) * TICKS, []):
+        push_all(which, t)
+    for t in range(2, far + 1):
+        push(last, t, 0)
         push(last, t, 1)
-        if t > 1:
-            push(last, t, 0)
-        if t == 1:
-            for part in parts_out(last - 1):
-                finish(last - 1, part)
+        if closing:
+            which = closing.pop(0)
+            for part in parts_out(which):
+                finish(which, part)
+    for which in closing:
+        for part in parts_out(which):
+            finish(which, part)
     finish(last, 0)
     finish(last, 1)
     for copy in moved.values():
@@ -396,6 +405,42 @@
     while prompt % size or resp % size:
         size //= 2
     return size
+
+
+def settle_kernel(*refs):
+    count = (len(refs) - 2) // 3
+    sources, targets, holds = refs[:count], refs[count : 2 * count], refs[2 * count : 3 * count]
+    taken, given = refs[3 * count :]
+    pieces = []
+    for i, (source, target, hold) in enumerate(zip(sources, targets, holds)):
+        chunks = 4 if source.size > 1 << 18 else 1
+        step = source.shape[-1] // chunks
+        for c in range(chunks):
+            cut = (slice(None),) * (len(source.shape) - 1) + (pl.ds(c * step, step),)
+            taking = pltpu.make_async_copy(source.at[cut], hold.at[cut], taken.at[i, c])
+            taking.start()
+            giving = pltpu.make_async_copy(hold.at[cut], target.at[cut], given.at[i, c])
+            pieces.append((taking, giving))
+    for taking, giving in pieces:
+        taking.wait()
+        giving.start()
+    for _, giving in pieces:
+        giving.wait()
+
+
+def settle(*arrays):
+    hbm = pl.BlockSpec(memory_space=pl.ANY)
+    dma = pltpu.SemaphoreType.DMA
+    return pl.pallas_call(
+        settle_kernel,
+        out_shape=tuple(jax.ShapeDtypeStruct(x.shape, x.dtype) for x in arrays),
+        in_specs=[hbm] * len(arrays),
+        out_specs=(hbm,) * len(arrays),
+        scratch_shapes=[pltpu.VMEM(x.shape, x.dtype) for x in arrays]
+        + [dma((len(arrays), 4)), dma((len(arrays), 4))],
+        compiler_params=pltpu.CompilerParams(vmem_limit_bytes=60 * MIB),
+        name="settle",
+    )(*arrays)
 
 
 def local(prompt_keys, prompt_values, queries, resp_keys, resp_values, cotangent, lengths):
@@ -451,7 +496,7 @@
         ),
         name="fused",
     )(lengths, prompt_keys, prompt_values, resp_keys, resp_values, queries, cotangent)
-    return gq, grk, grv, gpk, gpv
+    return settle(gq, grk, grv, gpk, gpv)
 
 
 def solution(mesh):

time: 88.3 us -> 73 us (0.83)
  Pallas kernels: 81.1 us -> 71 us
  local copies, waits for them, and re-layouts: 5.34 us -> 0 us
    pallas_call x1, Pallas kernels: 81.1 us -> 68.3 us  [local(): pl.pallas_call(functools.partial(fused_kernel, n, block), out_shape=(shap...]
    unnamed x13 -> x0, local copies, waits for them, and re-layouts: 5.34 us -> none
    pallas_call x0 -> x1, Pallas kernels: none -> 2.65 us  [settle(): pl.pallas_call(settle_kernel, out_shape=tuple((jax.ShapeDtypeStruct(x.sha...]
where the time goes in v1:
time: 73 us; the launch traced here: 71.8 us
  Pallas kernels  71 us (97%)
  between operations  0.8 us (1%)
    pallas_call x1, Pallas kernels, local(): pl.pallas_call(functools.partial(fused_kernel, n, block), out_shape=(shap...  68.3 us
    pallas_call x1, Pallas kernels, settle(): pl.pallas_call(settle_kernel, out_shape=tuple((jax.ShapeDtypeStruct(x.sha...  2.65 us

profile of v1, /device:TPU:3, one launch (start us, length us, event | category | flops | bytes accessed | tf_op | source)
XLA Modules:
  0.0 71.8 jit_solution(5121013213253839687)
XLA Ops:
  0.6 68.3 %fused.1 = (f32[2,48,4096]{2,1,0:T(8,128)}, f32[2,48,512]{2,1,0:T(8,128)}, f32[2,48,512]{2,1,0:T(8,128)}, f32[32,512]{1,0:T(8,128)}, f32[32,512]{1,0:T(8,128)}) custom-call(s32[2]{0:T(128)} %lengths.1, bf16[32,512]{1,0:T(8,128)(2,1)} %pk.1, bf16[32,512]{1,0:T(8,128)(2,1)} %pv.1, bf16[2,48,512]{2,1,0:T(8,128)(2,1)} %rk.1, bf16[2,48,512]{2,1,0:T(8,128)(2,1)} %rv.1, ...), custom_call_target="tpu_custom_call" | custom-call | tf_op jit(solution)/shard_map/fused/pallas_call | solution.py:462
  69.0 2.6 %settle.1 = (f32[2,48,4096]{2,1,0:T(8,128)}, f32[2,48,512]{2,1,0:T(8,128)}, f32[2,48,512]{2,1,0:T(8,128)}, f32[32,512]{1,0:T(8,128)}, f32[32,512]{1,0:T(8,128)}) custom-call(f32[2,48,4096]{2,1,0:T(8,128)} %get-tuple-element.10.refs_0_, f32[2,48,512]{2,1,0:T(8,128)} %get-tuple-element.11.refs_1_, f32[2,48,512]{2,1,0:T(8,128)} %get-tuple-element.12.refs_2_, ...), custom_call_target="tpu_custom_call" | custom-call | tf_op jit(solution)/shard_map/settle/pallas_call | solution.py:434

commit v2 on v1

--- a/solution.py
+++ b/solution.py
@@ -334,7 +334,7 @@
     last = len(units) - 1
     far = n // 2
     pulls = [(w - t + 1, t) for w in range(last + far) for t in range(1, far + 1) if 0 <= w - t + 1 <= last]
-    pulls.sort(key=lambda hop: (hop[0] + hop[1], hop[1]))
+    pulls.sort(key=lambda hop: (2 * hop[0] + hop[1], hop[1]))
 
     def advance(count):
         for _ in range(min(count, len(pulls))):
@@ -346,7 +346,7 @@
         copy.wait()
     advance(first - 1)
     pulled(0)
-    per_tick = -(-len(pulls) // 6)
+    per_tick = -(-len(pulls) // 12)
     due = {}
     for unit in range(last):
         for t in range(1, far + 1):

time: 73 us -> 72.5 us (level)
  no operation moved by 1% of the time
where the time goes in v2:
time: 72.5 us; the launch traced here: 71.4 us
  Pallas kernels  70.6 us (97%)
  between operations  0.8 us (1%)
    pallas_call x1, Pallas kernels, local(): pl.pallas_call(functools.partial(fused_kernel, n, block), out_shape=(shap...  68 us
    pallas_call x1, Pallas kernels, settle(): pl.pallas_call(settle_kernel, out_shape=tuple((jax.ShapeDtypeStruct(x.sha...  2.65 us

profile of v2, /device:TPU:3, one launch (start us, length us, event | category | flops | bytes accessed | tf_op | source)
XLA Modules:
  0.0 71.4 jit_solution(7606673904554135281)
XLA Ops:
  0.6 68.0 %fused.1 = (f32[2,48,4096]{2,1,0:T(8,128)}, f32[2,48,512]{2,1,0:T(8,128)}, f32[2,48,512]{2,1,0:T(8,128)}, f32[32,512]{1,0:T(8,128)}, f32[32,512]{1,0:T(8,128)}) custom-call(s32[2]{0:T(128)} %lengths.1, bf16[32,512]{1,0:T(8,128)(2,1)} %pk.1, bf16[32,512]{1,0:T(8,128)(2,1)} %pv.1, bf16[2,48,512]{2,1,0:T(8,128)(2,1)} %rk.1, bf16[2,48,512]{2,1,0:T(8,128)(2,1)} %rv.1, ...), custom_call_target="tpu_custom_call" | custom-call | tf_op jit(solution)/shard_map/fused/pallas_call | solution.py:462
  68.6 2.6 %settle.1 = (f32[2,48,4096]{2,1,0:T(8,128)}, f32[2,48,512]{2,1,0:T(8,128)}, f32[2,48,512]{2,1,0:T(8,128)}, f32[32,512]{1,0:T(8,128)}, f32[32,512]{1,0:T(8,128)}) custom-call(f32[2,48,4096]{2,1,0:T(8,128)} %get-tuple-element.10.refs_0_, f32[2,48,512]{2,1,0:T(8,128)} %get-tuple-element.11.refs_1_, f32[2,48,512]{2,1,0:T(8,128)} %get-tuple-element.12.refs_2_, ...), custom_call_target="tpu_custom_call" | custom-call | tf_op jit(solution)/shard_map/settle/pallas_call | solution.py:434
